TPU v7x, 32 devices: a whole 2x2x4 slice. The times are simulated.
32 devices in a mesh: groups: 2 (over y), range: 8 (over z, x), sub: 2 (over core).
Axes of the slice: x: 2, y: 2, z: 4, core: 2. Of those that a mesh axis runs over, the one named last changes fastest.
Arguments:
- samples: float32 [2, 1024, 32, 128], P(None, ('groups', 'range', 'sub')), parts along dimension 1, may hold values from -6 to 6
- beam_weights: float32 [32, 8, 2, 64, 128], P(('groups', 'range'), None, None, None, 'sub'), parts along dimension 0, may hold values from -0.25 to 0.25
- subarrays: int32 [32, 8, 64], P(('groups', 'range', 'sub')), parts along dimension 0, may hold values from 0 to 511, as said below
- training: int32 [64], P(('groups', 'range', 'sub')), parts along dimension 0, may hold values 0 or 1
Outputs:
- covariance: float32 [32, 8, 64, 128], P(('groups', 'range', 'sub')), parts along dimension 0
- filtered: float32 [2, 128, 64, 128], P(None, None, ('groups', 'range', 'sub')), parts along dimension 2
- energy: float32 [256], P('groups'), parts along dimension 0
There are 2 independent parts, one for each index of `groups`. A program takes and returns all parts, laid end to end along the dimension named above; each array names one. Nothing has to cross between parts.
Inputs may be any that keep to these rules, and one draw needn't show every extreme that they name: `subarrays`: in each gate block the 512 indices are all 512 channels, each once.
All inputs are finite; a program needn't handle non-finite values. No bound on the sum of `training` on one device may be relied on, other than what follows from the above.
Results may differ from a plain program's by a relative error of at most 0.0003.
Values sent between devices are 32-bit elements; how exact they have to be, the bound alone decides.
A program may use at most 64 MiB of HBM per device.

v0:
```python
import jax
import jax.numpy as jnp
from jax import lax
from jax.sharding import PartitionSpec as P

GB = 2
loading = 0.05


def block_terms(snaps, chosen, weights, masked, factor):
    highest = lax.Precision.HIGHEST
    picked = jnp.take(snaps, chosen, axis=1)
    real_part = picked[0]
    imag_part = picked[1]
    real_masked = real_part * masked
    imag_masked = imag_part * masked
    cov_real = (
        jnp.einsum("snx,smx->snm", real_masked, real_part, precision=highest)
        + jnp.einsum("snx,smx->snm", imag_masked, imag_part, precision=highest)
    ) * factor
    cov_imag = (
        jnp.einsum("snx,smx->snm", imag_masked, real_part, precision=highest)
        - jnp.einsum("snx,smx->snm", real_masked, imag_part, precision=highest)
    ) * factor
    w_real = weights[:, 0]
    w_imag = weights[:, 1]
    out_real = jnp.einsum("snk,snx->kx", w_real, real_part, precision=highest) + jnp.einsum(
        "snk,snx->kx", w_imag, imag_part, precision=highest
    )
    out_imag = jnp.einsum("snk,snx->kx", w_real, imag_part, precision=highest) - jnp.einsum(
        "snk,snx->kx", w_imag, real_part, precision=highest
    )
    prod_real = jnp.einsum("snm,smk->snk", cov_real, w_real, precision=highest) - jnp.einsum(
        "snm,smk->snk", cov_imag, w_imag, precision=highest
    )
    prod_imag = jnp.einsum("snm,smk->snk", cov_real, w_imag, precision=highest) + jnp.einsum(
        "snm,smk->snk", cov_imag, w_real, precision=highest
    )
    quadratic = jnp.sum(w_real * prod_real + w_imag * prod_imag, axis=(0, 1))
    inverse = 1.0 / jnp.sqrt(quadratic + loading)
    filtered = jnp.stack([out_real * inverse[:, None], out_imag * inverse[:, None]])
    energy = jnp.sum(out_real * out_real + out_imag * out_imag, axis=1)
    covariance = jnp.concatenate([cov_real, cov_imag], axis=-1)
    return (covariance, filtered, energy)


def body(samples, beam_weights, subarrays, training):
    range_count = lax.axis_size("range")
    core_count = lax.axis_size("sub")
    parts_iq, chan_dev, all_gates, pulses = samples.shape
    gate_dev = all_gates // (range_count * core_count)
    channels = chan_dev * range_count * core_count
    blocks_dev = gate_dev // GB
    spread = samples.reshape(parts_iq, 1, 1, chan_dev, range_count, core_count, gate_dev, pulses)
    turned = lax.all_to_all(
        lax.all_to_all(spread, "range", split_axis=4, concat_axis=1, tiled=True),
        "sub",
        split_axis=5,
        concat_axis=2,
        tiled=True,
    )
    local_data = turned.reshape(parts_iq, channels, blocks_dev, GB * pulses).transpose(2, 0, 1, 3)
    mine = lax.all_to_all(beam_weights, "sub", split_axis=0, concat_axis=4, tiled=True)
    gates_on = training.astype(jnp.float32).reshape(blocks_dev, GB)
    masked = jnp.repeat(gates_on, pulses, axis=1)
    factor = 1.0 / (GB * pulses)
    covs, filts, energies = jax.vmap(block_terms, in_axes=(0, 0, 0, 0, None))(
        local_data, subarrays, mine, masked, factor
    )
    beams = filts.shape[2]
    filtered = filts.reshape(blocks_dev, parts_iq, beams, GB, pulses).transpose(1, 2, 0, 3, 4)
    filtered = filtered.reshape(parts_iq, beams, gate_dev, pulses)
    total = lax.psum(jnp.sum(energies, axis=0), ("range", "sub"))
    energy = total / (all_gates * pulses)
    return (covs, filtered, energy)


def solution(mesh):
    placed = (
        P(None, ("groups", "range", "sub"), None, None),
        P(("groups", "range"), None, None, None, "sub"),
        P(("groups", "range", "sub"), None, None),
        P(("groups", "range", "sub")),
    )
    return jax.shard_map(
        body,
        mesh=mesh,
        in_specs=placed,
        out_specs=(
            P(("groups", "range", "sub"), None, None, None),
            P(None, None, ("groups", "range", "sub"), None),
            P("groups"),
        ),
        check_vma=False,
    )
```

profile of v0, /device:TPU:0, one launch (start us, length us, event | category | flops | bytes accessed | tf_op | source)
XLA Modules:
  0.0 92.5 jit_solution(9004139148378862796)
XLA Ops:
  0.6 0.0 copy-start
  0.6 2.5 %reshape.157 = f32[2,1,65536]{2,1,0:T(1,128)} reshape(f32[2,8,2,64,64]{4,3,2,1,0:T(8,128)} %param.5) | data formatting | bytes 1048576
  3.2 3.5 %all-to-all-start.2 = ((f32[2,1,65536]{2,1,0:T(1,128)}), f32[2,1,65536]{2,1,0:T(1,128)S(1)}, u32[]{:S(2)}, u32[]{:S(2)}) async-start(f32[2,1,65536]{2,1,0:T(1,128)} %reshape.157), calls=%async_computation.2 | async-start | bytes 1048576 | tf_op jit(solution)/shard_map/all_to_all | solution.py:63
  6.6 0.0 copy-done
  6.7 1.6 %copy.24 = f32[2,1,1,32,8,2,2,128]{7,6,3,5,0,2,1,4:T(2,128)} copy(f32[2,1,1,32,8,2,2,128]{7,6,5,4,3,0,2,1:T(2,128)S(1)} %bitcast.103) | data formatting | bytes 2097152 | tf_op jit(solution)/shard_map/reshape | solution.py:54
  8.2 0.0 copy-start.2
  8.2 0.2 all-to-all-done.2
  8.4 0.0 copy-start.1
  8.4 7.4 %all-to-all-start = ((f32[2,1,1,32,8,2,2,128]{7,6,3,5,0,2,1,4:T(2,128)}), f32[2,1,1,32,8,2,2,128]{7,6,3,5,0,2,1,4:T(2,128)S(1)}, u32[]{:S(2)}, u32[]{:S(2)}) async-start(f32[2,1,1,32,8,2,2,128]{7,6,3,5,0,2,1,4:T(2,128)} %copy.24), calls=%async_computation | async-start | bytes 2097152 | tf_op jit(solution)/shard_map/all_to_all | solution.py:56
  15.8 0.0 copy-done.2
  15.8 0.0 copy-done.1
  15.9 0.1 reshape.147
  15.9 0.5 broadcast.75
  16.4 2.3 %reduce.5 = f32[2,65536]{1,0:T(2,128)S(1)} reduce(f32[2,1,65536]{2,1,0:T(1,128)S(1)} %all-to-all-done.2, f32[]{:T(128)} %broadcast.75), dimensions={1}, to_apply=%all_to_all.44.reduce_sub_computation | reduce | bytes 1048580 | tf_op jit(solution)/shard_map/all_to_all | solution.py:63
  18.8 0.6 reshape.158
  19.4 1.9 %copy.29 = f32[1,8,2,64,2,64]{5,4,3,1,2,0:T(2,128)} copy(f32[1,8,2,64,2,64]{5,3,2,1,4,0:T(8,128)S(1)} %bitcast.98) | data formatting | bytes 1048576 | tf_op jit(solution)/shard_map/all_to_all | solution.py:63
  21.2 1.8 %all_to_all.47 = f32[1,8,2,64,128]{4,3,1,2,0:T(8,128)S(1)} reshape(f32[1,8,2,64,2,64]{5,4,3,1,2,0:T(2,128)} %copy.29) | data formatting | bytes 1048576 | tf_op jit(solution)/shard_map/all_to_all | solution.py:63
  23.1 0.1 broadcast_bitcast_fusion
  23.1 18.9 %all-to-all-done = f32[2,1,1,32,8,2,2,128]{7,6,3,5,0,2,1,4:T(2,128)S(1)} async-done(((f32[2,1,1,32,8,2,2,128]{7,6,3,5,0,2,1,4:T(2,128)}), f32[2,1,1,32,8,2,2,128]{7,6,3,5,0,2,1,4:T(2,128)S(1)}, u32[]{:S(2)}, u32[]{:S(2)}) %all-to-all-start) | async-done | bytes 1048608 | tf_op jit(solution)/shard_map/all_to_all | solution.py:56
  42.1 0.1 copy.25
  42.1 4.6 %all_to_all.51 = f32[2,8,1,32,1,2,2,128]{7,6,3,1,0,4,2,5:T(2,128)S(1)} all-to-all(f32[2,8,1,32,1,2,2,128]{7,6,3,1,0,4,2,5:T(2,128)S(1)} %copy.25), channel_id=1, replica_groups=mesh['groups'=2,'range'=8,'sub'=2] {'sub'}, dimensions={5} | all-to-all | bytes 2097152 | tf_op jit(solution)/shard_map/all_to_all | solution.py:55
  46.7 0.1 copy.26
  46.8 0.8 copy.27
  47.6 2.3 %gather_fusion = f32[512,2,256]{2,1,0:T(2,128)S(1)} fusion(f32[1,2,512,256]{3,1,2,0:T(2,128)S(1)} %copy.27, s32[512]{0:T(512)S(1)} %reshape.147), kind=kCustom, calls=%fused_computation | custom fusion | bytes 2101248 | tf_op jit(solution)/shard_map/vmap(jit(_take))/gather | solution.py:12
  50.0 0.1 copy.28
  50.1 0.1 broadcast_select_fusion
  50.2 1.0 %convolution_bitcast_fusion.2 = f32[256,128]{1,0:T(8,128)S(1)} fusion(f32[1,2,8,64,256]{4,3,2,1,0:T(8,128)S(1)} %broadcast_select_fusion, f32[1,8,2,64,128]{4,3,1,2,0:T(8,128)S(1)} %all_to_all.47), kind=kOutput, calls=%fused_computation.13 | convolution fusion | flops 201326592 | bytes 917504 | tf_op jit(solution)/shard_map/vmap(snk,snx->kx)/dot_general | solution.py:27
  51.2 1.0 %convolution_bitcast_fusion = f32[256,128]{1,0:T(8,128)S(1)} fusion(f32[1,2,8,64,256]{4,3,2,1,0:T(8,128)S(1)} %broadcast_select_fusion, f32[1,8,2,64,128]{4,3,1,2,0:T(8,128)S(1)} %all_to_all.47), kind=kOutput, calls=%fused_computation.11 | convolution fusion | flops 201326592 | bytes 917504 | tf_op jit(solution)/shard_map/vmap(snk,snx->kx)/dot_general | solution.py:30
  52.2 0.6 fusion.12
  52.9 0.6 fusion.2
  53.5 0.4 fusion.19
  53.9 0.4 fusion.18
  54.3 0.6 fusion.8
  54.9 1.0 %fusion.6 = f32[256,128]{1,0:T(8,128)S(1)} fusion(f32[256,128]{1,0:T(8,128)S(1)} %convolution_bitcast_fusion.2, f32[1,2,8,64,256]{4,3,2,1,0:T(8,128)S(1)} %broadcast_select_fusion, f32[1,8,2,64,128]{4,3,1,2,0:T(8,128)S(1)} %all_to_all.47), kind=kOutput, calls=%fused_computation.15 | convolution fusion | flops 201359360 | bytes 1048576 | tf_op jit(solution)/shard_map/vmap(snk,snx->kx)/dot_general | solution.py:27
  55.9 0.6 fusion.3
  56.5 0.4 fusion
  56.9 0.4 fusion.5
  57.4 1.0 %add_reduce_fusion = (f32[128]{0:T(128)S(1)}, f32[256,128]{1,0:T(8,128)S(1)}, f32[256,128]{1,0:T(8,128)S(1)}) fusion(f32[256,128]{1,0:T(8,128)S(1)} %fusion.6, f32[128]{0:T(128)S(1)} %add_rsqrt_fusion, f32[256,128]{1,0:T(8,128)S(1)} %convolution_bitcast_fusion, f32[1,8,2,64,128]{4,3,1,2,0:T(8,128)S(1)} %all_to_all.47, ...), kind=kOutput, calls=%fused_computation.36 | convolution fusion | flops 201555840 | bytes 1311744 | tf_op jit(solution)/shard_map/vmap(snk,snx->kx)/dot_general | solution.py:30
  58.4 31.6 %psum.7 = f32[128]{0:T(128)S(1)} all-reduce(f32[128]{0:T(128)S(1)} %get-tuple-element.3), channel_id=1, replica_groups=mesh['groups'=2,'range'=8,'sub'=2] {'range','sub'}, use_global_device_ids=true, to_apply=%region_2.3 | all-reduce | flops 128 | bytes 1024 | tf_op jit(solution)/shard_map/psum | solution.py:73
  90.1 0.5 broadcast_multiply_fusion.2
  90.6 0.1 copy.30
  90.7 0.1 copy.31
  90.8 0.8 pad_maximum_fusion
  91.7 0.8 pad_maximum_fusion.1
  (6 shorter events, 0.0 us)
Async XLA Ops:
  0.6 6.0 %copy-start = (f32[2,32,32,128]{3,2,1,0:T(8,128)S(1)}, f32[2,32,32,128]{3,2,1,0:T(8,128)}, u32[]{:S(2)}) copy-start(f32[2,32,32,128]{3,2,1,0:T(8,128)} %param.4) | copy-start | bytes 3145732
  3.2 5.2 %all-to-all-start.2 = ((f32[2,1,65536]{2,1,0:T(1,128)}), f32[2,1,65536]{2,1,0:T(1,128)S(1)}, u32[]{:S(2)}, u32[]{:S(2)}) async-start(f32[2,1,65536]{2,1,0:T(1,128)} %reshape.157), calls=%async_computation.2 | async-start | bytes 1048576 | tf_op jit(solution)/shard_map/all_to_all | solution.py:63
  8.2 7.6 %copy-start.2 = (s32[2]{0:T(128)S(1)}, s32[2]{0:T(128)}, u32[]{:S(2)}) copy-start(s32[2]{0:T(128)} %param.7) | copy-start | bytes 28
  8.4 7.4 %copy-start.1 = (s32[1,8,64]{2,1,0:T(8,128)S(1)}, s32[1,8,64]{2,1,0:T(8,128)}, u32[]{:S(2)}) copy-start(s32[1,8,64]{2,1,0:T(8,128)} %param.6) | copy-start | bytes 6148
  8.4 33.7 %all-to-all-start = ((f32[2,1,1,32,8,2,2,128]{7,6,3,5,0,2,1,4:T(2,128)}), f32[2,1,1,32,8,2,2,128]{7,6,3,5,0,2,1,4:T(2,128)S(1)}, u32[]{:S(2)}, u32[]{:S(2)}) async-start(f32[2,1,1,32,8,2,2,128]{7,6,3,5,0,2,1,4:T(2,128)} %copy.24), calls=%async_computation | async-start | bytes 2097152 | tf_op jit(solution)/shard_map/all_to_all | solution.py:56
where the time goes:
time: 92.9 us; the launch traced here: 92.5 us
  blocking collectives  36.2 us (39%)
  waiting for transfers between devices  19.1 us (21%)
  local copies, waits for them, and re-layouts  12.7 us (14%)
  starting transfers between devices  10.9 us (12%)
  matrix products  8.13 us (9%)
  other arithmetic  4.67 us (5%)
    psum x1, blocking collectives, body(): total = lax.psum(jnp.sum(energies, axis=0), ('range', 'sub'))  31.6 us
    all_to_all x1, waiting for transfers between devices, body(): lax.all_to_all(spread, 'range', split_axis=4, concat_axis=1, tiled=True)  18.9 us
    all_to_all x1, starting transfers between devices, body(): lax.all_to_all(spread, 'range', split_axis=4, concat_axis=1, tiled=True)  7.41 us
    all_to_all x1, blocking collectives, body(): lax.all_to_all(lax.all_to_all(spread, 'range', split_axis=4, concat_axis=...  4.58 us
    all_to_all x3, local copies, waits for them, and re-layouts, body(): lax.all_to_all(beam_weights, 'sub', split_axis=0, concat_axis=4, tiled=True)  4.18 us
    all_to_all x1, starting transfers between devices, body(): lax.all_to_all(beam_weights, 'sub', split_axis=0, concat_axis=4, tiled=True)  3.49 us
    unnamed x8, local copies, waits for them, and re-layouts  3.15 us
    gather x4, local copies, waits for them, and re-layouts, block_terms(): picked = jnp.take(snaps, chosen, axis=1)  2.5 us
  transfers between devices with their start and end apart: 2, of which 2 were waited for; matrix products, arithmetic and copies ran while one was open for 8% of the time, Pallas kernels for 0%

commit v1 on v0

--- a/solution.py
+++ b/solution.py
@@ -53,7 +53,12 @@
     blocks_dev = gate_dev // GB
     spread = samples.reshape(parts_iq, 1, 1, chan_dev, range_count, core_count, gate_dev, pulses)
     turned = lax.all_to_all(
-        lax.all_to_all(spread, "range", split_axis=4, concat_axis=1, tiled=True),
+        jnp.concatenate(
+            lax.all_to_all(
+                jnp.stack(jnp.split(spread, lax.axis_size("range"), axis=4)), "range", 0, 0
+            ),
+            axis=1,
+        ),
         "sub",
         split_axis=5,
         concat_axis=2,

time: 92.9 us -> 93.9 us (1.011)
  local copies, waits for them, and re-layouts: 12.7 us -> 14.2 us
    another operation x0 -> x2, local copies, waits for them, and re-layouts: none -> 1.82 us  [body(): jnp.stack(jnp.split(spread, lax.axis_size('range'), axis=4))]
    reshape x1, local copies, waits for them, and re-layouts: 1.56 us -> 0.07 us  [body(): jnp.concatenate(lax.all_to_all(jnp.stack(jnp.split(spread, lax.axis_size(...]
    unnamed x8 -> x16, local copies, waits for them, and re-layouts: 3.15 us -> 4.41 us
  transfers between devices with their start and end apart: 2 -> 2, of which waited for: 2 -> 1; matrix products, arithmetic and copies ran while one was open for 8% -> 9% of each run, Pallas kernels for 0% -> 0%
where the time goes in v1:
time: 93.9 us; the launch traced here: 93.5 us
  blocking collectives  36.2 us (39%)
  waiting for transfers between devices  18.5 us (20%)
  local copies, waits for them, and re-layouts  14.2 us (15%)
  starting transfers between devices  10.9 us (12%)
  matrix products  8.13 us (9%)
  other arithmetic  4.67 us (5%)
    psum x1, blocking collectives, body(): total = lax.psum(jnp.sum(energies, axis=0), ('range', 'sub'))  31.6 us
    all_to_all x1, waiting for transfers between devices, body(): lax.all_to_all(jnp.stack(jnp.split(spread, lax.axis_size('range'), axis=4...  18.5 us
    all_to_all x1, starting transfers between devices, body(): lax.all_to_all(jnp.stack(jnp.split(spread, lax.axis_size('range'), axis=4...  7.41 us
    all_to_all x1, blocking collectives, body(): lax.all_to_all(jnp.concatenate(lax.all_to_all(jnp.stack(jnp.split(spread,...  4.58 us
    unnamed x16, local copies, waits for them, and re-layouts  4.41 us
    all_to_all x3, local copies, waits for them, and re-layouts, body(): lax.all_to_all(beam_weights, 'sub', split_axis=0, concat_axis=4, tiled=True)  4.18 us
    all_to_all x1, starting transfers between devices, body(): lax.all_to_all(beam_weights, 'sub', split_axis=0, concat_axis=4, tiled=True)  3.49 us
    gather x4, local copies, waits for them, and re-layouts, block_terms(): picked = jnp.take(snaps, chosen, axis=1)  2.5 us
  transfers between devices with their start and end apart: 2, of which 1 were waited for; matrix products, arithmetic and copies ran while one was open for 9% of the time, Pallas kernels for 0%

profile of v1, /device:TPU:0, one launch (start us, length us, event | category | flops | bytes accessed | tf_op | source)
XLA Modules:
  0.0 93.5 jit_solution(8387221588690152034)
XLA Ops:
  0.6 0.0 copy-start
  0.6 2.5 %reshape.165 = f32[2,1,65536]{2,1,0:T(1,128)} reshape(f32[2,8,2,64,64]{4,3,2,1,0:T(8,128)} %param.5) | data formatting | bytes 1048576
  3.2 3.5 %all-to-all-start.2 = ((f32[2,1,65536]{2,1,0:T(1,128)}), f32[2,1,65536]{2,1,0:T(1,128)S(1)}, u32[]{:S(2)}, u32[]{:S(2)}) async-start(f32[2,1,65536]{2,1,0:T(1,128)} %reshape.165), calls=%async_computation.2 | async-start | bytes 1048576 | tf_op jit(solution)/shard_map/all_to_all | solution.py:68
  6.6 0.0 copy-done
  6.7 0.6 copy.37
  7.4 1.8 %copy.45 = f32[8,2,1,1,32,1,2,2,128]{8,7,4,6,1,5,3,2,0:T(2,128)} copy(f32[8,2,1,1,32,1,2,2,128]{8,4,7,6,1,5,3,2,0:T(8,128)S(1)} %fusion.20) | data formatting | bytes 2097152 | tf_op jit(solution)/shard_map/stack | solution.py:58
  9.2 0.0 copy-start.1
  9.2 0.0 all-to-all-done.2
  9.2 7.4 %all-to-all-start = ((f32[8,2,1,1,32,1,2,2,128]{8,7,4,6,1,5,3,2,0:T(2,128)}), f32[8,2,1,1,32,1,2,2,128]{8,7,4,6,1,5,3,2,0:T(2,128)S(1)}, u32[]{:S(2)}, u32[]{:S(2)}) async-start(f32[8,2,1,1,32,1,2,2,128]{8,7,4,6,1,5,3,2,0:T(2,128)} %copy.45), calls=%async_computation | async-start | bytes 2097152 | tf_op jit(solution)/shard_map/all_to_all | solution.py:57
  16.7 0.0 copy-done.1
  16.7 0.0 copy-start.2
  16.7 0.1 reshape.155
  16.8 0.6 copy-done.2
  17.4 0.5 broadcast.75
  17.9 2.3 %reduce.5 = f32[2,65536]{1,0:T(2,128)S(1)} reduce(f32[2,1,65536]{2,1,0:T(1,128)S(1)} %all-to-all-done.2, f32[]{:T(128)} %broadcast.75), dimensions={1}, to_apply=%all_to_all.31.reduce_sub_computation | reduce | bytes 1048580 | tf_op jit(solution)/shard_map/all_to_all | solution.py:68
  20.2 0.6 reshape.166
  20.8 1.9 %copy.50 = f32[1,8,2,64,2,64]{5,4,3,1,2,0:T(2,128)} copy(f32[1,8,2,64,2,64]{5,3,2,1,4,0:T(8,128)S(1)} %bitcast.150) | data formatting | bytes 1048576 | tf_op jit(solution)/shard_map/all_to_all | solution.py:68
  22.7 1.8 %all_to_all.34 = f32[1,8,2,64,128]{4,3,1,2,0:T(8,128)S(1)} reshape(f32[1,8,2,64,2,64]{5,4,3,1,2,0:T(2,128)} %copy.50) | data formatting | bytes 1048576 | tf_op jit(solution)/shard_map/all_to_all | solution.py:68
  24.5 0.1 broadcast_bitcast_fusion
  24.6 18.5 %all-to-all-done = f32[8,2,1,1,32,1,2,2,128]{8,7,4,6,1,5,3,2,0:T(2,128)S(1)} async-done(((f32[8,2,1,1,32,1,2,2,128]{8,7,4,6,1,5,3,2,0:T(2,128)}), f32[8,2,1,1,32,1,2,2,128]{8,7,4,6,1,5,3,2,0:T(2,128)S(1)}, u32[]{:S(2)}, u32[]{:S(2)}) %all-to-all-start) | async-done | bytes 1048608 | tf_op jit(solution)/shard_map/all_to_all | solution.py:57
  43.1 0.1 copy.46
  43.1 4.6 %all_to_all.38 = f32[2,8,1,32,1,2,2,128]{7,6,3,1,0,4,2,5:T(2,128)S(1)} all-to-all(f32[2,8,1,32,1,2,2,128]{7,6,3,1,0,4,2,5:T(2,128)S(1)} %copy.46), channel_id=1, replica_groups=mesh['groups'=2,'range'=8,'sub'=2] {'sub'}, dimensions={5} | all-to-all | bytes 2097152 | tf_op jit(solution)/shard_map/all_to_all | solution.py:55
  47.7 0.1 copy.47
  47.8 0.8 copy.48
  48.6 2.3 %gather_fusion = f32[512,2,256]{2,1,0:T(2,128)S(1)} fusion(f32[1,2,512,256]{3,1,2,0:T(2,128)S(1)} %copy.48, s32[512]{0:T(512)S(1)} %reshape.155), kind=kCustom, calls=%fused_computation | custom fusion | bytes 2101248 | tf_op jit(solution)/shard_map/vmap(jit(_take))/gather | solution.py:12
  51.0 0.1 copy.49
  51.1 0.1 broadcast_select_fusion
  51.2 0.6 fusion.12
  51.9 0.6 fusion.8
  52.5 0.6 fusion.2
  53.1 0.4 fusion.19
  53.5 0.4 fusion.18
  53.9 1.0 %convolution_bitcast_fusion.2 = f32[256,128]{1,0:T(8,128)S(1)} fusion(f32[1,2,8,64,256]{4,3,2,1,0:T(8,128)S(1)} %broadcast_select_fusion, f32[1,8,2,64,128]{4,3,1,2,0:T(8,128)S(1)} %all_to_all.34), kind=kOutput, calls=%fused_computation.13 | convolution fusion | flops 201326592 | bytes 917504 | tf_op jit(solution)/shard_map/vmap(snk,snx->kx)/dot_general | solution.py:27
  54.9 1.0 %convolution_bitcast_fusion = f32[256,128]{1,0:T(8,128)S(1)} fusion(f32[1,2,8,64,256]{4,3,2,1,0:T(8,128)S(1)} %broadcast_select_fusion, f32[1,8,2,64,128]{4,3,1,2,0:T(8,128)S(1)} %all_to_all.34), kind=kOutput, calls=%fused_computation.11 | convolution fusion | flops 201326592 | bytes 917504 | tf_op jit(solution)/shard_map/vmap(snk,snx->kx)/dot_general | solution.py:30
  55.9 0.6 fusion.3
  56.6 0.4 fusion
  57.0 0.4 fusion.5
  57.4 1.0 %fusion.6 = f32[256,128]{1,0:T(8,128)S(1)} fusion(f32[256,128]{1,0:T(8,128)S(1)} %convolution_bitcast_fusion.2, f32[1,2,8,64,256]{4,3,2,1,0:T(8,128)S(1)} %broadcast_select_fusion, f32[1,8,2,64,128]{4,3,1,2,0:T(8,128)S(1)} %all_to_all.34), kind=kOutput, calls=%fused_computation.15 | convolution fusion | flops 201359360 | bytes 1048576 | tf_op jit(solution)/shard_map/vmap(snk,snx->kx)/dot_general | solution.py:27
  58.4 1.0 %add_reduce_fusion = (f32[128]{0:T(128)S(1)}, f32[256,128]{1,0:T(8,128)S(1)}, f32[256,128]{1,0:T(8,128)S(1)}) fusion(f32[256,128]{1,0:T(8,128)S(1)} %fusion.6, f32[128]{0:T(128)S(1)} %add_rsqrt_fusion, f32[256,128]{1,0:T(8,128)S(1)} %convolution_bitcast_fusion, f32[1,8,2,64,128]{4,3,1,2,0:T(8,128)S(1)} %all_to_all.34, ...), kind=kOutput, calls=%fused_computation.52 | convolution fusion | flops 201555840 | bytes 1311744 | tf_op jit(solution)/shard_map/vmap(snk,snx->kx)/dot_general | solution.py:30
  59.4 0.1 copy.51
  59.6 0.1 copy.52
  59.7 31.6 %psum.7 = f32[128]{0:T(128)S(1)} all-reduce(f32[128]{0:T(128)S(1)} %get-tuple-element.3), channel_id=1, replica_groups=mesh['groups'=2,'range'=8,'sub'=2] {'range','sub'}, use_global_device_ids=true, to_apply=%region_2.3 | all-reduce | flops 128 | bytes 1024 | tf_op jit(solution)/shard_map/psum | solution.py:78
  91.3 0.5 broadcast_multiply_fusion.2
  91.8 0.8 pad_maximum_fusion.1
  92.7 0.8 pad_maximum_fusion
  (14 shorter events, 0.1 us)
Async XLA Ops:
  0.6 6.0 %copy-start = (f32[2,32,32,128]{3,2,1,0:T(8,128)S(1)}, f32[2,32,32,128]{3,2,1,0:T(8,128)}, u32[]{:S(2)}) copy-start(f32[2,32,32,128]{3,2,1,0:T(8,128)} %param.4) | copy-start | bytes 3145732
  3.2 6.1 %all-to-all-start.2 = ((f32[2,1,65536]{2,1,0:T(1,128)}), f32[2,1,65536]{2,1,0:T(1,128)S(1)}, u32[]{:S(2)}, u32[]{:S(2)}) async-start(f32[2,1,65536]{2,1,0:T(1,128)} %reshape.165), calls=%async_computation.2 | async-start | bytes 1048576 | tf_op jit(solution)/shard_map/all_to_all | solution.py:68
  9.2 7.4 %copy-start.1 = (s32[1,8,64]{2,1,0:T(8,128)S(1)}, s32[1,8,64]{2,1,0:T(8,128)}, u32[]{:S(2)}) copy-start(s32[1,8,64]{2,1,0:T(8,128)} %param.6) | copy-start | bytes 6148
  9.2 33.8 %all-to-all-start = ((f32[8,2,1,1,32,1,2,2,128]{8,7,4,6,1,5,3,2,0:T(2,128)}), f32[8,2,1,1,32,1,2,2,128]{8,7,4,6,1,5,3,2,0:T(2,128)S(1)}, u32[]{:S(2)}, u32[]{:S(2)}) async-start(f32[8,2,1,1,32,1,2,2,128]{8,7,4,6,1,5,3,2,0:T(2,128)} %copy.45), calls=%async_computation | async-start | bytes 2097152 | tf_op jit(solution)/shard_map/all_to_all | solution.py:57
  16.7 0.7 copy-start.2
